TPU v7x, 32 devices: a whole 2x2x4 slice. The times are simulated.
32 devices in a mesh: dp: 8 (over y, x, core), mp: 4 (over z).
Axes of the slice: x: 2, y: 2, z: 4, core: 2. Of those that a mesh axis runs over, the one named last changes fastest.
Arguments:
- tokens: bfloat16 [1024, 8192], P(('dp', 'mp')), parts along dimension 0, may hold values from -6 to 6
- norm_gain: float32 [8192], replicated, may hold values from 0.5 to 1.5
- qkv_weight: bfloat16 [8192, 10240], P(None, 'mp'), may hold values from -0.0625 to 0.0625
- qkv_bias: float32 [10240], P('mp'), may hold values from -3 to 3
- qkv_grad: bfloat16 [1024, 10240], P('dp', 'mp'), parts along dimension 0, may hold values from -6 to 6
Outputs:
- qkv: bfloat16 [1024, 10240], P('dp', 'mp'), parts along dimension 0
- tokens_grad: float32 [1024, 8192], P(('dp', 'mp')), parts along dimension 0
- gain_grad: float32 [65536], P('dp'), parts along dimension 0
- bias_grad: float32 [81920], P(('dp', 'mp')), parts along dimension 0
There are 8 independent parts, one for each index of `dp`. A program takes and returns all parts, laid end to end along the dimension named above; an argument that names none is the same for every part. Nothing has to cross between parts.
All inputs are finite; a program needn't handle non-finite values.
Results may differ from a plain program's by a relative error of at most 0.0046.
Values may be sent and summed in bfloat16 or wider, within the bound.
A program may use at most 128 MiB of HBM per device.

v0:
```python
import jax
import jax.numpy as jnp
from jax import lax
from jax.sharding import PartitionSpec as P

HEAD_DIM = 128
SEQ_LEN = 32768
GROUP = 10
TOK_DEV = 32


def rotate_heads(joined, first_col, position, sign):
    rows, cols = joined.shape
    heads = cols // HEAD_DIM
    half = HEAD_DIM // 2
    parts = joined.reshape(rows, heads, 2, half)
    inverse = jnp.exp(
        -jnp.log(jnp.float32(1000000.0)) * (2.0 * jnp.arange(half).astype(jnp.float32) / HEAD_DIM)
    )
    angle = position.astype(jnp.float32)[:, None] * inverse[None, :]
    cosine = jnp.cos(angle)[:, None, :]
    sine = sign * jnp.sin(angle)[:, None, :]
    first = parts[:, :, 0, :]
    second = parts[:, :, 1, :]
    turned = jnp.stack([first * cosine - second * sine, second * cosine + first * sine], axis=2)
    head_index = first_col // HEAD_DIM + jnp.arange(heads)
    rotated = head_index % GROUP != GROUP - 1
    result = jnp.where(rotated[None, :, None, None], turned, parts)
    return result.reshape(rows, cols)


def positions(rows, stride):
    row_index = jnp.arange(rows)
    return row_index // TOK_DEV * stride + row_index % TOK_DEV


def normalize(tokens, norm_gain):
    values = tokens.astype(jnp.float32)
    scale = lax.rsqrt(jnp.mean(values * values, axis=1, keepdims=True) + 1e-06)
    return (values * scale * norm_gain[None, :]).astype(jnp.bfloat16)


def shards(tokens, norm_gain, qkv_weight, qkv_bias, qkv_grad):
    width = qkv_weight.shape[1]
    first_col = lax.axis_index("mp") * width
    stride = SEQ_LEN // lax.axis_size("mp")
    place = positions(qkv_grad.shape[0], stride)
    joined_grad = rotate_heads(qkv_grad.astype(jnp.float32), first_col, place, -1.0)
    bias_grad = jnp.sum(joined_grad, axis=0)
    joined_low = joined_grad.astype(jnp.bfloat16)
    normed_grad = lax.psum_scatter(
        lax.dot_general(
            joined_low, qkv_weight, (((1,), (1,)), ((), ())), preferred_element_type=jnp.float32
        ),
        "mp",
        scatter_dimension=0,
        tiled=True,
    )
    values = tokens.astype(jnp.float32)
    scale = lax.rsqrt(jnp.mean(values * values, axis=1, keepdims=True) + 1e-06)
    gain_grad = lax.psum(jnp.sum(normed_grad * values * scale, axis=0), "mp")
    inner = jnp.mean(norm_gain[None, :] * normed_grad * values, axis=1, keepdims=True)
    tokens_grad = scale * norm_gain[None, :] * normed_grad - values * scale * scale * scale * inner
    tokens_grad, gain_grad, bias_grad = (tokens_grad, gain_grad, bias_grad)
    tokens_grad, later = lax.optimization_barrier((tokens_grad, tokens))
    normed = normalize(later, norm_gain)
    project_normed = lax.all_gather(normed, "mp", axis=0, tiled=True)
    joined = (
        jnp.dot(project_normed, qkv_weight, preferred_element_type=jnp.float32) + qkv_bias[None, :]
    )
    place = positions(project_normed.shape[0], stride)
    qkv = rotate_heads(joined, first_col, place, 1.0).astype(jnp.bfloat16)
    return (qkv, tokens_grad, gain_grad, bias_grad)


def solution(mesh):
    in_specs = (P(("dp", "mp"), None), P(), P(None, "mp"), P("mp"), P("dp", "mp"))
    out_specs = (P("dp", "mp"), P(("dp", "mp"), None), P("dp"), P(("dp", "mp")))
    return jax.shard_map(shards, mesh=mesh, in_specs=in_specs, out_specs=out_specs, check_vma=False)
```

profile of v0, /device:TPU:0, one launch (start us, length us, event | category | flops | bytes accessed | tf_op | source)
XLA Modules:
  0.0 186.8 jit_solution(11591648086676076548)
XLA Ops:
  7.2 0.0 reduce-scatter.2.cloned.1.call-start
  7.3 0.1 broadcast_in_dim.15
  7.4 0.1 broadcast_in_dim.16
  7.5 1.3 copy.9
  8.8 0.2 multiply_sine_fusion
  9.0 0.2 multiply_subtract_fusion.1
  9.2 0.1 pad_maximum_fusion
  9.4 0.0 copy-start.1
  9.4 0.4 copy.10
  9.8 0.7 copy-done.1
  10.5 20.4 %fusion.11 = f32[128,8192]{1,0:T(8,128)} fusion(bf16[8192,2560]{1,0:T(8,128)(2,1)} %param.7, f32[128,2560]{1,0:T(8,128)S(1)} %copy.10, pred[2560]{0:T(1024)(128)(4,1)S(1)} %broadcast_in_dim.16, bf16[128,2560]{1,0:T(8,128)(2,1)S(1)} %copy-done.1), kind=kOutput, calls=%fused_computation.23 | convolution fusion | flops 5369364480 | bytes 48105984 | tf_op jit(solution)/shard_map/dot_general | solution.py:52
  30.9 0.0 reduce-scatter.2.cloned.1.call-update
  30.9 0.0 all-gather.2.cloned.1.call-start
  31.0 1.0 copy-done
  32.0 0.2 fusion.3
  32.2 78.4 %reduce-scatter.2.cloned.1.call-done = f32[32,8192]{1,0:T(8,128)} async-done(((f32[128,8192]{1,0:T(8,128)}), f32[32,8192]{1,0:T(8,128)}) %reduce-scatter.2.cloned.1.call-update) | async-done | bytes 1048592 | tf_op jit(solution)/shard_map/reduce_scatter | solution.py:51
  110.6 0.0 copy-done.3
  110.6 1.7 fusion.10
  112.3 1.3 fusion.7
  113.7 0.2 fusion
  113.9 1.0 fusion.2
  114.9 0.0 all-gather.2.cloned.1.call-update
  114.9 0.8 fusion.13
  115.7 19.8 %psum.7 = f32[8192]{0:T(1024)} all-reduce(f32[8192]{0:T(1024)S(1)} %get-tuple-element.8), channel_id=1, replica_groups=mesh['dp'=8,'mp'=4] {'mp'}, use_global_device_ids=true, to_apply=%region_5.6 | all-reduce | flops 8192 | bytes 65536 | tf_op jit(solution)/shard_map/psum | solution.py:61
  135.5 26.1 %all-gather.2.cloned.1.call-done = bf16[128,8192]{1,0:T(8,128)(2,1)} async-done(((bf16[32,8192]{1,0:T(8,128)(2,1)}), bf16[128,8192]{1,0:T(8,128)(2,1)}) %all-gather.2.cloned.1.call-update) | async-done | bytes 2097168 | tf_op jit(solution)/shard_map/all_gather | solution.py:67
  161.6 0.0 copy-done.4
  161.6 16.4 %convolution_add_fusion = f32[128,2560]{1,0:T(8,128)S(1)} fusion(bf16[128,8192]{1,0:T(8,128)(2,1)} %all-gather.2.cloned.1.call-done, bf16[8192,2560]{1,0:T(8,128)(2,1)} %param.7, f32[2560]{0:T(1024)S(1)} %copy-done.4), kind=kOutput, calls=%fused_computation | convolution fusion | flops 5369036800 | bytes 45361152 | tf_op jit(solution)/shard_map/dot_general | solution.py:69
  178.0 0.4 copy.11
  178.4 0.2 multiply_subtract_fusion
  178.6 0.1 pad_maximum_fusion.1
  178.7 0.2 copy.12
  179.0 1.0 select_convert_fusion
  (11 shorter events, 0.1 us)
Async XLA Ops:
  7.2 103.4 %reduce-scatter.2.cloned.1.call-start = ((), (), s32[]{:S(2)}) async-start(), calls=%async_computation.1 | async-start | bytes 5242880 | tf_op jit(solution)/shard_map/reduce_scatter | solution.py:51
  9.4 1.1 copy-start.1
  30.9 1.0 copy-start
  30.9 79.7 %copy-start.3 = (f32[8192]{0:T(1024)S(1)}, f32[8192]{0:T(1024)}, u32[]{:S(2)}) copy-start(f32[8192]{0:T(1024)} %param.6) | copy-start | bytes 98308
  30.9 130.7 %all-gather.2.cloned.1.call-start = ((), (), s32[]{:S(2)}) async-start(), calls=%async_computation.2 | async-start | bytes 2621440 | tf_op jit(solution)/shard_map/all_gather | solution.py:67
  110.6 1.7 copy-start.2
  114.9 46.7 %copy-start.4 = (f32[2560]{0:T(1024)S(1)}, f32[2560]{0:T(1024)}, u32[]{:S(2)}) copy-start(f32[2560]{0:T(1024)} %param.8) | copy-start | bytes 30724
Sparse Core Ops, SparseCore 0:
  31.1 79.5 reduce-scatter.1
  115.0 46.5 all-gather.1
where the time goes:
time: 187 us
  waiting for transfers between devices  105 us (56%)
  matrix products  36.9 us (20%)
  blocking collectives  19.8 us (11%)
  between operations  14.2 us (8%)
  other arithmetic  7.08 us (4%)
  local copies, waits for them, and re-layouts  4.19 us (2%)
    reduce_scatter x1, waiting for transfers between devices, shards(): lax.psum_scatter(lax.dot_general(joined_low, qkv_weight, (((1,), (1,)), (...  78.4 us
    all_gather x1, waiting for transfers between devices, shards(): project_normed = lax.all_gather(normed, 'mp', axis=0, tiled=True)  26.1 us
    dot_general x1, matrix products, shards(): lax.dot_general(joined_low, qkv_weight, (((1,), (1,)), ((), ())), preferr...  20.4 us
    psum x1, blocking collectives, shards(): gain_grad = lax.psum(jnp.sum(normed_grad * values * scale, axis=0), 'mp')  19.8 us
    dot_general x1, matrix products, shards(): jnp.dot(project_normed, qkv_weight, preferred_element_type=jnp.float32)  16.4 us
  transfers between devices with their start and end apart: 2, of which 2 were waited for; matrix products, arithmetic and copies ran while one was open for 1% of the time, Pallas kernels for 0%

commit v1 on v0

v1 whole, which is shorter than its diff:
```python
import functools

import jax
import jax.numpy as jnp
import numpy as np
from jax import lax
from jax.experimental import pallas as pl
from jax.experimental.pallas import tpu as pltpu
from jax.sharding import PartitionSpec as P

HEAD_DIM = 128
SEQ_LEN = 32768
GROUP = 10
CHUNKS = 4
TILE_K = 512
MESH = pl.DeviceIdType.MESH


def rope_tables(rows, tok_dev, stride):
    half = HEAD_DIM // 2
    row = np.arange(rows)
    place = (row // tok_dev * stride + row % tok_dev).astype(np.float32)
    inverse = np.exp(
        -np.log(np.float32(1000000.0))
        * (np.float32(2.0) * np.arange(half).astype(np.float32) / np.float32(HEAD_DIM))
    ).astype(np.float32)
    angle = (place[:, None] * inverse[None, :]).astype(np.float32)
    cosine, sine = np.cos(angle).astype(np.float32), np.sin(angle).astype(np.float32)
    return np.concatenate([cosine, cosine], 1), np.concatenate([-sine, sine], 1)


def kernel(
    n,
    tok_h, gain_h, w_h, bias_h, grad_h, cos_h, sin_h,
    qkv_h, tg_h, gg_ref, bg_ref,
    tok, gain, w, bias, grad, cos, sin,
    low, part, held, run, acc, qkv, ng, tg, scale_ref, gsend, grecv,
    in_sem, w_sem, out_sem, send_sem, recv_sem, gsend_sem, grecv_sem,
):
    me = lax.axis_index("mp")
    rows, depth = tok.shape
    width = w.shape[1]
    heads = width // HEAD_DIM
    span = depth // CHUNKS
    tiles = depth // TILE_K
    per = tiles // CHUNKS
    f32 = jnp.float32

    loads = []
    for i, (src, dst) in enumerate(
        ((tok_h, tok), (gain_h, gain), (grad_h, grad), (cos_h, cos), (sin_h, sin), (bias_h, bias))
    ):
        c = pltpu.make_async_copy(src, dst, in_sem.at[i])
        c.start()
        loads.append(c)

    def w_copy(i):
        k = pl.ds(pl.multiple_of(i * TILE_K, TILE_K), TILE_K)
        return pltpu.make_async_copy(w_h.at[k, :], w.at[k, :], w_sem.at[i])

    @pl.loop(0, tiles)
    def _(i):
        w_copy(i).start()

    barrier = pltpu.get_barrier_semaphore()
    for k in range(1, n):
        pl.semaphore_signal(
            barrier, inc=1, device_id={"mp": lax.rem(me + k, n)}, device_id_type=MESH
        )

    def block(s):
        return pl.ds(pl.multiple_of(s * rows, rows), rows)

    def cols(c):
        return pl.ds(pl.multiple_of(c * span, span), span)

    loads[0].wait()
    loads[1].wait()
    total = jnp.zeros((rows, 1), f32)
    for c in range(CHUNKS):
        v = tok[:, c * span:(c + 1) * span].astype(f32)
        total = total + jnp.sum(v * v, axis=1, keepdims=True)
    scale = lax.rsqrt(total / depth + 1e-06)
    scale_ref[...] = jnp.broadcast_to(scale, scale_ref.shape)
    for c in range(CHUNKS):
        ks = slice(c * span, (c + 1) * span)
        held[block(me), ks] = (tok[:, ks].astype(f32) * scale * gain[:, ks]).astype(jnp.bfloat16)
    pl.semaphore_wait(barrier, n - 1)

    def transfer(way, buf, at, j, c):
        ref = buf.at[block(at), cols(c)]
        return pltpu.make_async_remote_copy(
            src_ref=ref,
            dst_ref=ref,
            send_sem=send_sem.at[way, j, c],
            recv_sem=recv_sem.at[way, j, c],
            device_id={"mp": lax.rem(me + (1 if way == 0 else n - 1), n)},
            device_id_type=MESH,
        )

    has_right, has_left = me < n - 1, me > 0

    def step(j, c):
        for way, goes, comes, back in ((0, has_right, has_left, me), (1, has_left, has_right, n - 1 - me)):
            @pl.when(comes)
            def _():
                transfer(way, held, 0, j - 1, c).wait_recv()

            @pl.when(goes)
            def _():
                @pl.when(j <= back)
                def _():
                    transfer(way, held, me - j if way == 0 else me + j, j, c).start()

                @pl.when(j > back)
                def _():
                    t = n - j + me if way == 0 else j - n + me
                    slot = t + 1 if way == 0 else t

                    @pl.when(comes)
                    def _():
                        value = part[block(t), cols(c)] + run[block(slot), cols(c)].astype(f32)
                        run[block(slot), cols(c)] = value.astype(jnp.bfloat16)

                    @pl.when(jnp.logical_not(comes))
                    def _():
                        run[block(slot), cols(c)] = part[block(t), cols(c)].astype(jnp.bfloat16)

                    transfer(way, run, slot, j, c).start()

    for c in range(CHUNKS):
        for way, goes in ((0, has_right), (1, has_left)):
            @pl.when(goes)
            def _():
                transfer(way, held, me, 0, c).start()

    for l in loads[2:]:
        l.wait()
    for h in range(heads):
        hs = slice(h * HEAD_DIM, (h + 1) * HEAD_DIM)
        x = grad[:, hs].astype(f32)
        turned = x * cos[...] - pltpu.roll(x, HEAD_DIM // 2, 1) * sin[...]
        plain = lax.rem(me * heads + h, GROUP) == GROUP - 1
        x = jnp.where(plain, x, turned)
        bg_ref[:, hs] = jnp.sum(x, axis=0, keepdims=True)
        low[:, hs] = x.astype(jnp.bfloat16)

    def backward(c):
        @pl.loop(0, per)
        def _(i):
            at = c * per + i
            w_copy(at).wait()
            k = pl.ds(pl.multiple_of(at * TILE_K, TILE_K), TILE_K)
            part[:, k] = lax.dot_general(
                low[...], w[k, :], (((1,), (1,)), ((), ())), preferred_element_type=f32
            )

    @pl.loop(0, CHUNKS)
    def _(c):
        backward(c)

        @pl.when(c > 0)
        def _():
            step(1, c - 1)

    step(1, CHUNKS - 1)

    @pl.loop(2, n - 1)
    def _(j):
        @pl.loop(0, CHUNKS)
        def _(c):
            step(j, c)

    tile_n = 640 if width % 640 == 0 else HEAD_DIM
    tiles_n = width // tile_n

    @pl.loop(0, CHUNKS)
    def _(c):
        step(n - 1, c)

        @pl.loop(0, tiles_n)
        def _(i):
            ns = pl.ds(pl.multiple_of(i * tile_n, tile_n), tile_n)
            value = jnp.dot(held[:, cols(c)], w[cols(c), ns], preferred_element_type=f32)

            @pl.when(c == 0)
            def _():
                acc[:, ns] = value

            @pl.when(c > 0)
            def _():
                acc[:, ns] += value

    for h in range(heads):
        hs = slice(h * HEAD_DIM, (h + 1) * HEAD_DIM)
        x = acc[:, hs] + bias[:, hs]
        turned = x * cos[...] + pltpu.roll(x, HEAD_DIM // 2, 1) * sin[...]
        plain = lax.rem(me * heads + h, GROUP) == GROUP - 1
        qkv[:, hs] = jnp.where(plain, x, turned).astype(jnp.bfloat16)
    out_q = pltpu.make_async_copy(qkv, qkv_h, out_sem.at[0])
    out_q.start()

    def gain_copy(k, c):
        return pltpu.make_async_remote_copy(
            src_ref=gsend.at[c],
            dst_ref=grecv.at[k - 1, c],
            send_sem=gsend_sem.at[k - 1, c],
            recv_sem=grecv_sem.at[k - 1, c],
            device_id={"mp": lax.rem(me + k, n)},
            device_id_type=MESH,
        )

    scale = scale_ref[:, :1]
    inner = jnp.zeros((rows, 1), f32)
    piece = span // 8
    for c in range(CHUNKS):
        ks = slice(c * span, (c + 1) * span)
        ng[:, ks] = part[block(me), ks]
        for way, comes, slot in ((0, has_left, me + 1), (1, has_right, me)):
            @pl.when(comes)
            def _():
                transfer(way, run, slot, n - 1, c).wait_recv()
                ng[:, ks] += run[block(slot), ks].astype(f32)

        product = ng[:, ks] * tok[:, ks].astype(f32)
        gg = jnp.sum(product * scale, axis=0, keepdims=True)
        inner = inner + jnp.sum(product * gain[:, ks], axis=1, keepdims=True)
        for i in range(8):
            gsend[c, i:i + 1, :] = gg[:, i * piece:(i + 1) * piece]
        for k in range(1, n):
            gain_copy(k, c).start()

    weight = scale * scale * scale * (inner / depth)
    for c in range(CHUNKS):
        ks = slice(c * span, (c + 1) * span)
        tg[:, ks] = scale * gain[:, ks] * ng[:, ks] - tok[:, ks].astype(f32) * weight
    out_t = pltpu.make_async_copy(tg, tg_h, out_sem.at[1])
    out_t.start()

    for c in range(CHUNKS):
        total = gsend[c]
        for k in range(1, n):
            gain_copy(k, c).wait_recv()
            total = total + grecv[k - 1, c]
        for i in range(8):
            at = c * span + i * piece
            gg_ref[:, at:at + piece] = total[i:i + 1, :]

    @pl.loop(0, n)
    def _(j):
        @pl.loop(0, CHUNKS)
        def _(c):
            for way, goes in ((0, has_right), (1, has_left)):
                @pl.when(goes)
                def _():
                    transfer(way, held, 0, j, c).wait_send()

    for c in range(CHUNKS):
        for k in range(1, n):
            gain_copy(k, c).wait_send()
    out_q.wait()
    out_t.wait()


def shards(n, tokens, norm_gain, qkv_weight, qkv_bias, qkv_grad):
    rows, depth = tokens.shape
    every, width = qkv_grad.shape
    cosine, sine = rope_tables(every, rows, SEQ_LEN // n)
    bf16, f32 = jnp.bfloat16, jnp.float32
    span = depth // CHUNKS
    dma = pltpu.SemaphoreType.DMA
    hbm = pl.BlockSpec(memory_space=pl.ANY)
    vmem = pl.BlockSpec(memory_space=pltpu.VMEM)
    qkv, tokens_grad, gain_grad, bias_grad = pl.pallas_call(
        functools.partial(kernel, n),
        out_shape=(
            jax.ShapeDtypeStruct((every, width), bf16),
            jax.ShapeDtypeStruct((rows, depth), f32),
            jax.ShapeDtypeStruct((1, depth), f32),
            jax.ShapeDtypeStruct((1, width), f32),
        ),
        in_specs=[hbm] * 7,
        out_specs=(hbm, hbm, vmem, vmem),
        scratch_shapes=[
            pltpu.VMEM((rows, depth), bf16),
            pltpu.VMEM((1, depth), f32),
            pltpu.VMEM((depth, width), bf16),
            pltpu.VMEM((1, width), f32),
            pltpu.VMEM((every, width), bf16),
            pltpu.VMEM((every, HEAD_DIM), f32),
            pltpu.VMEM((every, HEAD_DIM), f32),
            pltpu.VMEM((every, width), bf16),
            pltpu.VMEM((every, depth), f32),
            pltpu.VMEM((every, depth), bf16),
            pltpu.VMEM((every + rows, depth), bf16),
            pltpu.VMEM((every, width), f32),
            pltpu.VMEM((every, width), bf16),
            pltpu.VMEM((rows, depth), f32),
            pltpu.VMEM((rows, depth), f32),
            pltpu.VMEM((rows, HEAD_DIM), f32),
            pltpu.VMEM((CHUNKS, 8, span // 8), f32),
            pltpu.VMEM((n - 1, CHUNKS, 8, span // 8), f32),
            dma((6,)),
            dma((depth // TILE_K,)),
            dma((2,)),
            dma((2, n, CHUNKS)),
            dma((2, n, CHUNKS)),
            dma((n - 1, CHUNKS)),
            dma((n - 1, CHUNKS)),
        ],
        compiler_params=pltpu.CompilerParams(
            collective_id=0, has_side_effects=True, vmem_limit_bytes=65000000
        ),
        cost_estimate=pl.CostEstimate(
            flops=4 * every * depth * width, bytes_accessed=2 * depth * width, transcendentals=0
        ),
    )(
        tokens, norm_gain.reshape(1, depth), qkv_weight, qkv_bias.reshape(1, width), qkv_grad,
        jnp.asarray(cosine), jnp.asarray(sine),
    )
    return qkv, tokens_grad, gain_grad.reshape(depth), bias_grad.reshape(width)


def solution(mesh):
    in_specs = (P(("dp", "mp"), None), P(), P(None, "mp"), P("mp"), P("dp", "mp"))
    out_specs = (P("dp", "mp"), P(("dp", "mp"), None), P("dp"), P(("dp", "mp")))
    body = functools.partial(shards, mesh.shape["mp"])
    return jax.shard_map(body, mesh=mesh, in_specs=in_specs, out_specs=out_specs, check_vma=False)
```

time: 187 us -> 66.1 us (0.35)
  waiting for transfers between devices: 105 us -> 0 us
  Pallas kernels: 0 us -> 56.9 us
  matrix products: 36.9 us -> 0 us
  blocking collectives: 19.8 us -> 0 us
  between operations: 14.2 us -> 0.64 us
  other arithmetic: 7.08 us -> 1.33 us
  local copies, waits for them, and re-layouts: 4.19 us -> 6.91 us
    reduce_scatter x1 -> x0, waiting for transfers between devices: 78.4 us -> none  [shards(): lax.psum_scatter(lax.dot_general(joined_low, qkv_weight, (((1,), (1,)), (...]
    pallas_call x0 -> x1, Pallas kernels: none -> 56.9 us  [shards(): pl.pallas_call(functools.partial(kernel, n), out_shape=(jax.ShapeDtypeStr...]
    dot_general x2 -> x0, matrix products: 36.9 us -> none  [the longest x1 20.4 us: shards(): lax.dot_general(joined_low, qkv_weight, (((1,), (1,)), ((), ())), preferr...]
    all_gather x1 -> x0, waiting for transfers between devices: 26.1 us -> none  [shards(): project_normed = lax.all_gather(normed, 'mp', axis=0, tiled=True)]
    psum x1 -> x0, blocking collectives: 19.8 us -> none  [shards(): gain_grad = lax.psum(jnp.sum(normed_grad * values * scale, axis=0), 'mp')]
    unnamed x10 -> x3, local copies, waits for them, and re-layouts: 1.66 us -> 5.6 us
    reduce_sum x4 -> x0, other arithmetic: 2.94 us -> none  [the longest x1 1.71 us: shards(): gain_grad = lax.psum(jnp.sum(normed_grad * values * scale, axis=0), 'mp')]
    convert_element_type x3 -> x0, other arithmetic: 1.95 us -> none  [the longest x1 0.99 us: normalize(): return (values * scale * norm_gain[None, :]).astype(jnp.bfloat16)]
  transfers between devices with their start and end apart: 2 -> 0, of which waited for: 2 -> 0; matrix products, arithmetic and copies ran while one was open for 1% -> 0% of each run, Pallas kernels for 0% -> 0%
where the time goes in v1:
time: 66.1 us; the launch traced here: 65.8 us
  Pallas kernels  56.9 us (86%)
  local copies, waits for them, and re-layouts  6.91 us (10%)
  other arithmetic  1.33 us (2%)
    pallas_call x1, Pallas kernels, shards(): pl.pallas_call(functools.partial(kernel, n), out_shape=(jax.ShapeDtypeStr...  56.9 us
    unnamed x3, local copies, waits for them, and re-layouts  5.6 us
    pallas_call x1, other arithmetic, shards(): pl.pallas_call(functools.partial(kernel, n), out_shape=(jax.ShapeDtypeStr...  1.33 us

profile of v1, /device:TPU:0, one launch (start us, length us, event | category | flops | bytes accessed | tf_op | source)
XLA Modules:
  0.0 65.8 jit_solution(7424761661488041943)
XLA Ops:
  0.6 1.3 %reshape.21.bias_h = f32[1,2560]{1,0:T(1,128)} reshape(f32[2560]{0:T(1024)} %param.10) | data formatting | bytes 20480 | tf_op jit(solution)/shard_map/reshape | solution.py:318
  1.9 56.9 %shard_map.102 = (bf16[128,2560]{1,0:T(8,128)(2,1)}, f32[32,8192]{1,0:T(8,128)}, f32[1,8192]{1,0:T(1,128)}, f32[1,2560]{1,0:T(1,128)}) custom-call(bf16[32,8192]{1,0:T(8,128)(2,1)} %tok_h.1, f32[1,8192]{1,0:T(1,128)} %bitcast.3, bf16[8192,2560]{1,0:T(8,128)(2,1)} %w_h.1, f32[1,2560]{1,0:T(1,128)} %reshape.21.bias_h, bf16[128,2560]{1,0:T(8,128)(2,1)} %grad_h.1, ...), custom_call_target="tpu_custom_call" | custom-call | flops 10737418240 | bytes 41943040 | tf_op jit(solution)/shard_map/pallas_call | solution.py:274
  58.8 1.3 %reduce = f32[2560]{0:T(1024)} reduce(f32[1,2560]{1,0:T(1,128)} %get-tuple-element.11, f32[]{:T(128)} %constant.6), dimensions={0}, to_apply=%get-tuple-element.11.reduce_sub_computation | reduce | bytes 20484 | tf_op jit(solution)/shard_map/pallas_call | solution.py:274
  60.2 2.0 %copy.14 = bf16[128,2560]{1,0:T(8,128)(2,1)} copy(bf16[128,2560]{1,0:T(8,128)(2,1)} %get-tuple-element.16) | data formatting | bytes 1310720
  62.1 2.3 %copy.15 = f32[32,8192]{1,0:T(8,128)} copy(f32[32,8192]{1,0:T(8,128)} %get-tuple-element.17) | data formatting | bytes 2097152
  64.4 1.4 %copy.16 = f32[8192]{0:T(1024)} copy(f32[8192]{0:T(1024)} %bitcast.2) | data formatting | bytes 65536

commit v2 on v1

--- a/solution.py
+++ b/solution.py
@@ -32,10 +32,10 @@
 def kernel(
     n,
     tok_h, gain_h, w_h, bias_h, grad_h, cos_h, sin_h,
-    qkv_h, tg_h, gg_ref, bg_ref,
+    qkv, tg, gg_ref, bg_ref,
     tok, gain, w, bias, grad, cos, sin,
-    low, part, held, run, acc, qkv, ng, tg, scale_ref, gsend, grecv,
-    in_sem, w_sem, out_sem, send_sem, recv_sem, gsend_sem, grecv_sem,
+    low, part, held, run, acc, ng, scale_ref, gsend, grecv,
+    in_sem, w_sem, send_sem, recv_sem, gsend_sem, grecv_sem,
 ):
     me = lax.axis_index("mp")
     rows, depth = tok.shape
@@ -48,7 +48,7 @@
 
     loads = []
     for i, (src, dst) in enumerate(
-        ((tok_h, tok), (gain_h, gain), (grad_h, grad), (cos_h, cos), (sin_h, sin), (bias_h, bias))
+        ((tok_h, tok), (gain_h, gain.at[0]), (grad_h, grad), (cos_h, cos), (sin_h, sin), (bias_h, bias.at[0]))
     ):
         c = pltpu.make_async_copy(src, dst, in_sem.at[i])
         c.start()
@@ -197,8 +197,6 @@
         turned = x * cos[...] + pltpu.roll(x, HEAD_DIM // 2, 1) * sin[...]
         plain = lax.rem(me * heads + h, GROUP) == GROUP - 1
         qkv[:, hs] = jnp.where(plain, x, turned).astype(jnp.bfloat16)
-    out_q = pltpu.make_async_copy(qkv, qkv_h, out_sem.at[0])
-    out_q.start()
 
     def gain_copy(k, c):
         return pltpu.make_async_remote_copy(
@@ -234,8 +232,6 @@
     for c in range(CHUNKS):
         ks = slice(c * span, (c + 1) * span)
         tg[:, ks] = scale * gain[:, ks] * ng[:, ks] - tok[:, ks].astype(f32) * weight
-    out_t = pltpu.make_async_copy(tg, tg_h, out_sem.at[1])
-    out_t.start()
 
     for c in range(CHUNKS):
         total = gsend[c]
@@ -258,8 +254,15 @@
     for c in range(CHUNKS):
         for k in range(1, n):
             gain_copy(k, c).wait_send()
-    out_q.wait()
-    out_t.wait()
+
+
+def finish(qkv, tg, gg, bg, qkv_h, tg_h, gg_h, bg_h, sem):
+    moves = ((qkv, qkv_h), (tg, tg_h), (gg.at[0], gg_h), (bg.at[0], bg_h))
+    copies = [pltpu.make_async_copy(src, dst, sem.at[i]) for i, (src, dst) in enumerate(moves)]
+    for c in copies:
+        c.start()
+    for c in copies:
+        c.wait()
 
 
 def shards(n, tokens, norm_gain, qkv_weight, qkv_bias, qkv_grad):
@@ -271,16 +274,16 @@
     dma = pltpu.SemaphoreType.DMA
     hbm = pl.BlockSpec(memory_space=pl.ANY)
     vmem = pl.BlockSpec(memory_space=pltpu.VMEM)
-    qkv, tokens_grad, gain_grad, bias_grad = pl.pallas_call(
+    results = pl.pallas_call(
         functools.partial(kernel, n),
         out_shape=(
-            jax.ShapeDtypeStruct((every, width), bf16),
-            jax.ShapeDtypeStruct((rows, depth), f32),
-            jax.ShapeDtypeStruct((1, depth), f32),
-            jax.ShapeDtypeStruct((1, width), f32),
+            pltpu.VMEM((every, width), bf16),
+            pltpu.VMEM((rows, depth), f32),
+            pltpu.VMEM((1, depth), f32),
+            pltpu.VMEM((1, width), f32),
         ),
         in_specs=[hbm] * 7,
-        out_specs=(hbm, hbm, vmem, vmem),
+        out_specs=[vmem] * 4,
         scratch_shapes=[
             pltpu.VMEM((rows, depth), bf16),
             pltpu.VMEM((1, depth), f32),
@@ -294,31 +297,40 @@
             pltpu.VMEM((every, depth), bf16),
             pltpu.VMEM((every + rows, depth), bf16),
             pltpu.VMEM((every, width), f32),
-            pltpu.VMEM((every, width), bf16),
-            pltpu.VMEM((rows, depth), f32),
             pltpu.VMEM((rows, depth), f32),
             pltpu.VMEM((rows, HEAD_DIM), f32),
             pltpu.VMEM((CHUNKS, 8, span // 8), f32),
             pltpu.VMEM((n - 1, CHUNKS, 8, span // 8), f32),
             dma((6,)),
             dma((depth // TILE_K,)),
-            dma((2,)),
             dma((2, n, CHUNKS)),
             dma((2, n, CHUNKS)),
             dma((n - 1, CHUNKS)),
             dma((n - 1, CHUNKS)),
         ],
         compiler_params=pltpu.CompilerParams(
-            collective_id=0, has_side_effects=True, vmem_limit_bytes=65000000
+            collective_id=0, has_side_effects=True, vmem_limit_bytes=60000000
         ),
         cost_estimate=pl.CostEstimate(
             flops=4 * every * depth * width, bytes_accessed=2 * depth * width, transcendentals=0
         ),
     )(
-        tokens, norm_gain.reshape(1, depth), qkv_weight, qkv_bias.reshape(1, width), qkv_grad,
+        tokens, norm_gain, qkv_weight, qkv_bias, qkv_grad,
         jnp.asarray(cosine), jnp.asarray(sine),
     )
-    return qkv, tokens_grad, gain_grad.reshape(depth), bias_grad.reshape(width)
+    return pl.pallas_call(
+        finish,
+        out_shape=(
+            jax.ShapeDtypeStruct((every, width), bf16),
+            jax.ShapeDtypeStruct((rows, depth), f32),
+            jax.ShapeDtypeStruct((depth,), f32),
+            jax.ShapeDtypeStruct((width,), f32),
+        ),
+        in_specs=[vmem] * 4,
+        out_specs=[hbm] * 4,
+        scratch_shapes=[dma((4,))],
+        compiler_params=pltpu.CompilerParams(vmem_limit_bytes=1 << 20),
+    )(*results)
 
 
 def solution(mesh):

time: 66.1 us -> 58.3 us (0.88)
  local copies, waits for them, and re-layouts: 6.91 us -> 0 us
  other arithmetic: 1.33 us -> 0 us
  Pallas kernels: 56.9 us -> 57.6 us
    unnamed x3 -> x0, local copies, waits for them, and re-layouts: 5.6 us -> none
    pallas_call x1 -> x0, other arithmetic: 1.33 us -> none  [shards(): pl.pallas_call(functools.partial(kernel, n), out_shape=(jax.ShapeDtypeStr...]
    reshape x1 -> x0, local copies, waits for them, and re-layouts: 1.31 us -> none  [shards(): qkv_bias.reshape(1, width)]
    pallas_call x1 -> x2, Pallas kernels: 56.9 us -> 57.6 us  [the longest x1 56.3 us: shards(): pl.pallas_call(functools.partial(kernel, n), out_shape=(pltpu.VMEM((every...]
where the time goes in v2:
time: 58.3 us; the launch traced here: 58.2 us
  Pallas kernels  57.6 us (99%)
  between operations  0.64 us (1%)
    pallas_call x1, Pallas kernels, shards(): pl.pallas_call(functools.partial(kernel, n), out_shape=(pltpu.VMEM((every...  56.3 us
    pallas_call x1, Pallas kernels, shards(): pl.pallas_call(finish, out_shape=(jax.ShapeDtypeStruct((every, width), bf...  1.23 us

profile of v2, /device:TPU:0, one launch (start us, length us, event | category | flops | bytes accessed | tf_op | source)
XLA Modules:
  0.0 58.2 jit_solution(16802115321279006316)
XLA Ops:
  0.6 56.3 %shard_map.102 = (bf16[128,2560]{1,0:T(8,128)(2,1)S(1)}, f32[32,8192]{1,0:T(8,128)S(1)}, f32[1,8192]{1,0:T(1,128)S(1)}, f32[1,2560]{1,0:T(1,128)S(1)}) custom-call(bf16[32,8192]{1,0:T(8,128)(2,1)} %tok_h.1, f32[8192]{0:T(1024)} %gain_h.1, bf16[8192,2560]{1,0:T(8,128)(2,1)} %w_h.1, f32[2560]{0:T(1024)} %bias_h.1, bf16[128,2560]{1,0:T(8,128)(2,1)} %grad_h.1, ...), custom_call_target="tpu_custom_call" | custom-call | flops 10737418240 | bytes 41943040 | tf_op jit(solution)/shard_map/pallas_call | solution.py:277
  57.0 1.2 %shard_map.103 = (bf16[128,2560]{1,0:T(8,128)(2,1)}, f32[32,8192]{1,0:T(8,128)}, f32[8192]{0:T(1024)}, f32[2560]{0:T(1024)}) custom-call(bf16[128,2560]{1,0:T(8,128)(2,1)S(1)} %get-tuple-element.8.qkv, f32[32,8192]{1,0:T(8,128)S(1)} %get-tuple-element.9.tg, f32[1,8192]{1,0:T(1,128)S(1)} %get-tuple-element.10.gg, f32[1,2560]{1,0:T(1,128)S(1)} %get-tuple-element.11.bg), custom_call_target="tpu_custom_call" | custom-call | tf_op jit(solution)/shard_map/pallas_call | solution.py:321

commit v3 on v2

--- a/solution.py
+++ b/solution.py
@@ -34,7 +34,7 @@
     tok_h, gain_h, w_h, bias_h, grad_h, cos_h, sin_h,
     qkv, tg, gg_ref, bg_ref,
     tok, gain, w, bias, grad, cos, sin,
-    low, part, held, run, acc, ng, scale_ref, gsend, grecv,
+    low, part, held, run, acc, ng, scale_ref, gmine, gsend, grecv,
     in_sem, w_sem, send_sem, recv_sem, gsend_sem, grecv_sem,
 ):
     me = lax.axis_index("mp")
@@ -46,6 +46,15 @@
     per = tiles // CHUNKS
     f32 = jnp.float32
 
+    has_right, has_left = me < n - 1, me > 0
+    barrier = pltpu.get_barrier_semaphore()
+    for there, k in ((has_right, 1), (has_left, n - 1)):
+        @pl.when(there)
+        def _():
+            pl.semaphore_signal(
+                barrier, inc=1, device_id={"mp": lax.rem(me + k, n)}, device_id_type=MESH
+            )
+
     loads = []
     for i, (src, dst) in enumerate(
         ((tok_h, tok), (gain_h, gain.at[0]), (grad_h, grad), (cos_h, cos), (sin_h, sin), (bias_h, bias.at[0]))
@@ -58,16 +67,6 @@
         k = pl.ds(pl.multiple_of(i * TILE_K, TILE_K), TILE_K)
         return pltpu.make_async_copy(w_h.at[k, :], w.at[k, :], w_sem.at[i])
 
-    @pl.loop(0, tiles)
-    def _(i):
-        w_copy(i).start()
-
-    barrier = pltpu.get_barrier_semaphore()
-    for k in range(1, n):
-        pl.semaphore_signal(
-            barrier, inc=1, device_id={"mp": lax.rem(me + k, n)}, device_id_type=MESH
-        )
-
     def block(s):
         return pl.ds(pl.multiple_of(s * rows, rows), rows)
 
@@ -85,7 +84,16 @@
     for c in range(CHUNKS):
         ks = slice(c * span, (c + 1) * span)
         held[block(me), ks] = (tok[:, ks].astype(f32) * scale * gain[:, ks]).astype(jnp.bfloat16)
-    pl.semaphore_wait(barrier, n - 1)
+    inside = has_right & has_left
+
+    @pl.when(inside)
+    def _():
+        pl.semaphore_wait(barrier, 2)
+
+    @pl.when(jnp.logical_not(inside))
+    def _():
+        pl.semaphore_wait(barrier, 1)
+
 
     def transfer(way, buf, at, j, c):
         ref = buf.at[block(at), cols(c)]
@@ -98,8 +106,6 @@
             device_id_type=MESH,
         )
 
-    has_right, has_left = me < n - 1, me > 0
-
     def step(j, c):
         for way, goes, comes, back in ((0, has_right, has_left, me), (1, has_left, has_right, n - 1 - me)):
             @pl.when(comes)
@@ -133,6 +139,10 @@
             @pl.when(goes)
             def _():
                 transfer(way, held, me, 0, c).start()
+
+    @pl.loop(0, tiles)
+    def _(i):
+        w_copy(i).start()
 
     for l in loads[2:]:
         l.wait()
@@ -174,30 +184,6 @@
     tile_n = 640 if width % 640 == 0 else HEAD_DIM
     tiles_n = width // tile_n
 
-    @pl.loop(0, CHUNKS)
-    def _(c):
-        step(n - 1, c)
-
-        @pl.loop(0, tiles_n)
-        def _(i):
-            ns = pl.ds(pl.multiple_of(i * tile_n, tile_n), tile_n)
-            value = jnp.dot(held[:, cols(c)], w[cols(c), ns], preferred_element_type=f32)
-
-            @pl.when(c == 0)
-            def _():
-                acc[:, ns] = value
-
-            @pl.when(c > 0)
-            def _():
-                acc[:, ns] += value
-
-    for h in range(heads):
-        hs = slice(h * HEAD_DIM, (h + 1) * HEAD_DIM)
-        x = acc[:, hs] + bias[:, hs]
-        turned = x * cos[...] + pltpu.roll(x, HEAD_DIM // 2, 1) * sin[...]
-        plain = lax.rem(me * heads + h, GROUP) == GROUP - 1
-        qkv[:, hs] = jnp.where(plain, x, turned).astype(jnp.bfloat16)
-
     def gain_copy(k, c):
         return pltpu.make_async_remote_copy(
             src_ref=gsend.at[c],
@@ -208,9 +194,44 @@
             device_id_type=MESH,
         )
 
+    piece = span // 16
+
+    @pl.loop(0, CHUNKS)
+    def _(c):
+        step(n - 1, c)
+        for i in range(16):
+            ks = pl.ds(pl.multiple_of(c * span + i * piece, piece), piece)
+            share = jnp.sum(part[:, ks] * held[:, ks].astype(f32), axis=0, keepdims=True)
+            gmine[c, i:i + 1, :] = share / gain[:, ks]
+        gsend[c] = gmine[c].astype(jnp.bfloat16)
+
+        @pl.loop(0, tiles_n)
+        def _(i):
+            ns = pl.ds(pl.multiple_of(i * tile_n, tile_n), tile_n)
+            value = jnp.dot(held[:, cols(c)], w[cols(c), ns], preferred_element_type=f32)
+
+            @pl.when(c == 0)
+            def _():
+                acc[:, ns] = value
+
+            @pl.when(c > 0)
+            def _():
+                acc[:, ns] += value
+
+            @pl.when(i == 0)
+            def _():
+                for k in range(1, n):
+                    gain_copy(k, c).start()
+
+    for h in range(heads):
+        hs = slice(h * HEAD_DIM, (h + 1) * HEAD_DIM)
+        x = acc[:, hs] + bias[:, hs]
+        turned = x * cos[...] + pltpu.roll(x, HEAD_DIM // 2, 1) * sin[...]
+        plain = lax.rem(me * heads + h, GROUP) == GROUP - 1
+        qkv[:, hs] = jnp.where(plain, x, turned).astype(jnp.bfloat16)
+
     scale = scale_ref[:, :1]
     inner = jnp.zeros((rows, 1), f32)
-    piece = span // 8
     for c in range(CHUNKS):
         ks = slice(c * span, (c + 1) * span)
         ng[:, ks] = part[block(me), ks]
@@ -221,12 +242,7 @@
                 ng[:, ks] += run[block(slot), ks].astype(f32)
 
         product = ng[:, ks] * tok[:, ks].astype(f32)
-        gg = jnp.sum(product * scale, axis=0, keepdims=True)
         inner = inner + jnp.sum(product * gain[:, ks], axis=1, keepdims=True)
-        for i in range(8):
-            gsend[c, i:i + 1, :] = gg[:, i * piece:(i + 1) * piece]
-        for k in range(1, n):
-            gain_copy(k, c).start()
 
     weight = scale * scale * scale * (inner / depth)
     for c in range(CHUNKS):
@@ -234,11 +250,11 @@
         tg[:, ks] = scale * gain[:, ks] * ng[:, ks] - tok[:, ks].astype(f32) * weight
 
     for c in range(CHUNKS):
-        total = gsend[c]
+        total = gmine[c]
         for k in range(1, n):
             gain_copy(k, c).wait_recv()
-            total = total + grecv[k - 1, c]
-        for i in range(8):
+            total = total + grecv[k - 1, c].astype(f32)
+        for i in range(16):
             at = c * span + i * piece
             gg_ref[:, at:at + piece] = total[i:i + 1, :]
 
@@ -299,8 +315,9 @@
             pltpu.VMEM((every, width), f32),
             pltpu.VMEM((rows, depth), f32),
             pltpu.VMEM((rows, HEAD_DIM), f32),
-            pltpu.VMEM((CHUNKS, 8, span // 8), f32),
-            pltpu.VMEM((n - 1, CHUNKS, 8, span // 8), f32),
+            pltpu.VMEM((CHUNKS, 16, span // 16), f32),
+            pltpu.VMEM((CHUNKS, 16, span // 16), bf16),
+            pltpu.VMEM((n - 1, CHUNKS, 16, span // 16), bf16),
             dma((6,)),
             dma((depth // TILE_K,)),
             dma((2, n, CHUNKS)),

time: 58.3 us -> 56.7 us (0.973)
  Pallas kernels: 57.6 us -> 55.9 us
    pallas_call x1, Pallas kernels: 56.3 us -> 54.7 us  [shards(): pl.pallas_call(functools.partial(kernel, n), out_shape=(pltpu.VMEM((every...]
where the time goes in v3:
time: 56.7 us; the launch traced here: 56.6 us
  Pallas kernels  55.9 us (99%)
  between operations  0.64 us (1%)
    pallas_call x1, Pallas kernels, shards(): pl.pallas_call(functools.partial(kernel, n), out_shape=(pltpu.VMEM((every...  54.7 us
    pallas_call x1, Pallas kernels, shards(): pl.pallas_call(finish, out_shape=(jax.ShapeDtypeStruct((every, width), bf...  1.23 us

profile of v3, /device:TPU:0, one launch (start us, length us, event | category | flops | bytes accessed | tf_op | source)
XLA Modules:
  0.0 56.6 jit_solution(15422798668568722165)
XLA Ops:
  0.6 54.7 %shard_map.102 = (bf16[128,2560]{1,0:T(8,128)(2,1)S(1)}, f32[32,8192]{1,0:T(8,128)S(1)}, f32[1,8192]{1,0:T(1,128)S(1)}, f32[1,2560]{1,0:T(1,128)S(1)}) custom-call(bf16[32,8192]{1,0:T(8,128)(2,1)} %tok_h.1, f32[8192]{0:T(1024)} %gain_h.1, bf16[8192,2560]{1,0:T(8,128)(2,1)} %w_h.1, f32[2560]{0:T(1024)} %bias_h.1, bf16[128,2560]{1,0:T(8,128)(2,1)} %grad_h.1, ...), custom_call_target="tpu_custom_call" | custom-call | flops 10737418240 | bytes 41943040 | tf_op jit(solution)/shard_map/pallas_call | solution.py:293
  55.3 1.2 %shard_map.103 = (bf16[128,2560]{1,0:T(8,128)(2,1)}, f32[32,8192]{1,0:T(8,128)}, f32[8192]{0:T(1024)}, f32[2560]{0:T(1024)}) custom-call(bf16[128,2560]{1,0:T(8,128)(2,1)S(1)} %get-tuple-element.8.qkv, f32[32,8192]{1,0:T(8,128)S(1)} %get-tuple-element.9.tg, f32[1,8192]{1,0:T(1,128)S(1)} %get-tuple-element.10.gg, f32[1,2560]{1,0:T(1,128)S(1)} %get-tuple-element.11.bg), custom_call_target="tpu_custom_call" | custom-call | tf_op jit(solution)/shard_map/pallas_call | solution.py:338

commit v4 on v3

--- a/solution.py
+++ b/solution.py
@@ -106,12 +106,14 @@
             device_id_type=MESH,
         )
 
-    def step(j, c):
+    def arrive(j, c):
+        for way, comes in ((0, has_left), (1, has_right)):
+            @pl.when(comes)
+            def _():
+                transfer(way, held, 0, j - 1, c).wait_recv()
+
+    def depart(j, c):
         for way, goes, comes, back in ((0, has_right, has_left, me), (1, has_left, has_right, n - 1 - me)):
-            @pl.when(comes)
-            def _():
-                transfer(way, held, 0, j - 1, c).wait_recv()
-
             @pl.when(goes)
             def _():
                 @pl.when(j <= back)
@@ -133,6 +135,10 @@
                         run[block(slot), cols(c)] = part[block(t), cols(c)].astype(jnp.bfloat16)
 
                     transfer(way, run, slot, j, c).start()
+
+    def step(j, c):
+        arrive(j, c)
+        depart(j, c)
 
     for c in range(CHUNKS):
         for way, goes in ((0, has_right), (1, has_left)):
@@ -184,12 +190,12 @@
     tile_n = 640 if width % 640 == 0 else HEAD_DIM
     tiles_n = width // tile_n
 
-    def gain_copy(k, c):
+    def gain_copy(k):
         return pltpu.make_async_remote_copy(
-            src_ref=gsend.at[c],
-            dst_ref=grecv.at[k - 1, c],
-            send_sem=gsend_sem.at[k - 1, c],
-            recv_sem=grecv_sem.at[k - 1, c],
+            src_ref=gsend,
+            dst_ref=grecv.at[k - 1],
+            send_sem=gsend_sem.at[k - 1],
+            recv_sem=grecv_sem.at[k - 1],
             device_id={"mp": lax.rem(me + k, n)},
             device_id_type=MESH,
         )
@@ -198,13 +204,20 @@
 
     @pl.loop(0, CHUNKS)
     def _(c):
-        step(n - 1, c)
+        arrive(n - 1, c)
         for i in range(16):
             ks = pl.ds(pl.multiple_of(c * span + i * piece, piece), piece)
             share = jnp.sum(part[:, ks] * held[:, ks].astype(f32), axis=0, keepdims=True)
             gmine[c, i:i + 1, :] = share / gain[:, ks]
         gsend[c] = gmine[c].astype(jnp.bfloat16)
 
+        @pl.when(c == CHUNKS - 1)
+        def _():
+            for k in range(1, n):
+                gain_copy(k).start()
+
+        depart(n - 1, c)
+
         @pl.loop(0, tiles_n)
         def _(i):
             ns = pl.ds(pl.multiple_of(i * tile_n, tile_n), tile_n)
@@ -217,11 +230,6 @@
             @pl.when(c > 0)
             def _():
                 acc[:, ns] += value
-
-            @pl.when(i == 0)
-            def _():
-                for k in range(1, n):
-                    gain_copy(k, c).start()
 
     for h in range(heads):
         hs = slice(h * HEAD_DIM, (h + 1) * HEAD_DIM)
@@ -249,10 +257,11 @@
         ks = slice(c * span, (c + 1) * span)
         tg[:, ks] = scale * gain[:, ks] * ng[:, ks] - tok[:, ks].astype(f32) * weight
 
+    for k in range(1, n):
+        gain_copy(k).wait_recv()
     for c in range(CHUNKS):
         total = gmine[c]
         for k in range(1, n):
-            gain_copy(k, c).wait_recv()
             total = total + grecv[k - 1, c].astype(f32)
         for i in range(16):
             at = c * span + i * piece
@@ -267,9 +276,8 @@
                 def _():
                     transfer(way, held, 0, j, c).wait_send()
 
-    for c in range(CHUNKS):
-        for k in range(1, n):
-            gain_copy(k, c).wait_send()
+    for k in range(1, n):
+        gain_copy(k).wait_send()
 
 
 def finish(qkv, tg, gg, bg, qkv_h, tg_h, gg_h, bg_h, sem):
@@ -322,8 +330,8 @@
             dma((depth // TILE_K,)),
             dma((2, n, CHUNKS)),
             dma((2, n, CHUNKS)),
-            dma((n - 1, CHUNKS)),
-            dma((n - 1, CHUNKS)),
+            dma((n - 1,)),
+            dma((n - 1,)),
         ],
         compiler_params=pltpu.CompilerParams(
             collective_id=0, has_side_effects=True, vmem_limit_bytes=60000000

time: 56.7 us -> 55 us (0.970)
  Pallas kernels: 55.9 us -> 54.2 us
    pallas_call x1, Pallas kernels: 54.7 us -> 53 us  [shards(): pl.pallas_call(functools.partial(kernel, n), out_shape=(pltpu.VMEM((every...]
where the time goes in v4:
time: 55 us; the launch traced here: 54.9 us
  Pallas kernels  54.2 us (99%)
  between operations  0.64 us (1%)
    pallas_call x1, Pallas kernels, shards(): pl.pallas_call(functools.partial(kernel, n), out_shape=(pltpu.VMEM((every...  53 us
    pallas_call x1, Pallas kernels, shards(): pl.pallas_call(finish, out_shape=(jax.ShapeDtypeStruct((every, width), bf...  1.23 us

profile of v4, /device:TPU:0, one launch (start us, length us, event | category | flops | bytes accessed | tf_op | source)
XLA Modules:
  0.0 54.9 jit_solution(8820748257148708654)
XLA Ops:
  0.6 53.0 %shard_map.102 = (bf16[128,2560]{1,0:T(8,128)(2,1)S(1)}, f32[32,8192]{1,0:T(8,128)S(1)}, f32[1,8192]{1,0:T(1,128)S(1)}, f32[1,2560]{1,0:T(1,128)S(1)}) custom-call(bf16[32,8192]{1,0:T(8,128)(2,1)} %tok_h.1, f32[8192]{0:T(1024)} %gain_h.1, bf16[8192,2560]{1,0:T(8,128)(2,1)} %w_h.1, f32[2560]{0:T(1024)} %bias_h.1, bf16[128,2560]{1,0:T(8,128)(2,1)} %grad_h.1, ...), custom_call_target="tpu_custom_call" | custom-call | flops 10737418240 | bytes 41943040 | tf_op jit(solution)/shard_map/pallas_call | solution.py:301
  53.6 1.2 %shard_map.103 = (bf16[128,2560]{1,0:T(8,128)(2,1)}, f32[32,8192]{1,0:T(8,128)}, f32[8192]{0:T(1024)}, f32[2560]{0:T(1024)}) custom-call(bf16[128,2560]{1,0:T(8,128)(2,1)S(1)} %get-tuple-element.8.qkv, f32[32,8192]{1,0:T(8,128)S(1)} %get-tuple-element.9.tg, f32[1,8192]{1,0:T(1,128)S(1)} %get-tuple-element.10.gg, f32[1,2560]{1,0:T(1,128)S(1)} %get-tuple-element.11.bg), custom_call_target="tpu_custom_call" | custom-call | tf_op jit(solution)/shard_map/pallas_call | solution.py:346

commit v5 on v4

--- a/solution.py
+++ b/solution.py
@@ -242,6 +242,16 @@
     inner = jnp.zeros((rows, 1), f32)
     for c in range(CHUNKS):
         ks = slice(c * span, (c + 1) * span)
+        if c == CHUNKS - 1:
+            for k in range(1, n):
+                gain_copy(k).wait_recv()
+            for g in range(CHUNKS):
+                total = gmine[g]
+                for k in range(1, n):
+                    total = total + grecv[k - 1, g].astype(f32)
+                for i in range(16):
+                    at = g * span + i * piece
+                    gg_ref[:, at:at + piece] = total[i:i + 1, :]
         ng[:, ks] = part[block(me), ks]
         for way, comes, slot in ((0, has_left, me + 1), (1, has_right, me)):
             @pl.when(comes)
@@ -251,21 +261,12 @@
 
         product = ng[:, ks] * tok[:, ks].astype(f32)
         inner = inner + jnp.sum(product * gain[:, ks], axis=1, keepdims=True)
+        tg[:, ks] = scale * gain[:, ks] * ng[:, ks]
 
     weight = scale * scale * scale * (inner / depth)
     for c in range(CHUNKS):
         ks = slice(c * span, (c + 1) * span)
-        tg[:, ks] = scale * gain[:, ks] * ng[:, ks] - tok[:, ks].astype(f32) * weight
-
-    for k in range(1, n):
-        gain_copy(k).wait_recv()
-    for c in range(CHUNKS):
-        total = gmine[c]
-        for k in range(1, n):
-            total = total + grecv[k - 1, c].astype(f32)
-        for i in range(16):
-            at = c * span + i * piece
-            gg_ref[:, at:at + piece] = total[i:i + 1, :]
+        tg[:, ks] -= tok[:, ks].astype(f32) * weight
 
     @pl.loop(0, n)
     def _(j):

time: 55 us -> 54.9 us (level)
  no operation moved by 1% of the time
where the time goes in v5:
time: 54.9 us; the launch traced here: 54.8 us
  Pallas kernels  54.1 us (99%)
  between operations  0.64 us (1%)
    pallas_call x1, Pallas kernels, shards(): pl.pallas_call(functools.partial(kernel, n), out_shape=(pltpu.VMEM((every...  52.9 us
    pallas_call x1, Pallas kernels, shards(): pl.pallas_call(finish, out_shape=(jax.ShapeDtypeStruct((every, width), bf...  1.23 us

profile of v5, /device:TPU:0, one launch (start us, length us, event | category | flops | bytes accessed | tf_op | source)
XLA Modules:
  0.0 54.8 jit_solution(11937480749961207466)
XLA Ops:
  0.6 52.9 %shard_map.102 = (bf16[128,2560]{1,0:T(8,128)(2,1)S(1)}, f32[32,8192]{1,0:T(8,128)S(1)}, f32[1,8192]{1,0:T(1,128)S(1)}, f32[1,2560]{1,0:T(1,128)S(1)}) custom-call(bf16[32,8192]{1,0:T(8,128)(2,1)} %tok_h.1, f32[8192]{0:T(1024)} %gain_h.1, bf16[8192,2560]{1,0:T(8,128)(2,1)} %w_h.1, f32[2560]{0:T(1024)} %bias_h.1, bf16[128,2560]{1,0:T(8,128)(2,1)} %grad_h.1, ...), custom_call_target="tpu_custom_call" | custom-call | flops 10737418240 | bytes 41943040 | tf_op jit(solution)/shard_map/pallas_call | solution.py:302
  53.5 1.2 %shard_map.103 = (bf16[128,2560]{1,0:T(8,128)(2,1)}, f32[32,8192]{1,0:T(8,128)}, f32[8192]{0:T(1024)}, f32[2560]{0:T(1024)}) custom-call(bf16[128,2560]{1,0:T(8,128)(2,1)S(1)} %get-tuple-element.8.qkv, f32[32,8192]{1,0:T(8,128)S(1)} %get-tuple-element.9.tg, f32[1,8192]{1,0:T(1,128)S(1)} %get-tuple-element.10.gg, f32[1,2560]{1,0:T(1,128)S(1)} %get-tuple-element.11.bg), custom_call_target="tpu_custom_call" | custom-call | tf_op jit(solution)/shard_map/pallas_call | solution.py:347
